TPU v7x, 32 devices: a whole 2x2x4 slice. The times are simulated.
32 devices in a mesh: seq: 8 (over z, x), dp: 4 (over y, core).
Axes of the slice: x: 2, y: 2, z: 4, core: 2. Of those that a mesh axis runs over, the one named last changes fastest.
Arguments:
- conv_input: bfloat16 [4, 2048, 2816], P('dp', 'seq'), may hold values from -6 to 6
- gate_input: bfloat16 [4, 2048, 2560], P('dp', 'seq'), may hold values from -6 to 6
- step_input: float32 [4, 40, 2048], P('dp', None, 'seq'), may hold values from -7.5 to 2048
- filter_taps: float32 [4, 2816], replicated, may hold values from -3 to 3
- filter_bias: float32 [2816], replicated, may hold values from -0.5 to 0.5
- step_bias: float32 [40], replicated, may hold values from -1 to 1
- decay_log: float32 [40], replicated, may hold values from -13 to 3
- skip_gain: float32 [40], replicated, may hold values from 0.5 to 1.5
- norm_weight: float32 [2560], replicated, may hold values from 0.5 to 1.5
- output_weight: bfloat16 [2560, 1280], P('dp'), may hold values from -0.125 to 0.125
- output_grad: bfloat16 [4, 2048, 1280], P('dp', 'seq'), may hold values from -6 to 6
Outputs:
- input_grad: bfloat16 [4, 2048, 2816], P('dp', 'seq')
- gate_grad: bfloat16 [4, 2048, 2560], P('dp', 'seq')
- step_grad: float32 [4, 40, 2048], P('dp', None, 'seq')
- weight_grad: float32 [2560, 1280], P('dp')
- filter_grads: float32 [5, 2816], replicated
- norm_grad: float32 [2560], replicated
- head_grads: float32 [3, 40], replicated
All inputs are finite; a program needn't handle non-finite values.
Results may differ from a plain program's by a relative error of at most 0.0029.
Values may be sent and summed in bfloat16 or wider, within the bound.
No kernel may reach another device: no remote copies, remote signals or barrier semaphores. Data moves between devices by JAX's collectives and lax.ppermute only.
A program may use at most 192 MiB of HBM per device.

v0:
```python
import jax
import jax.numpy as jnp
from jax import lax
from jax.sharding import PartitionSpec as P

HEADS = 40
HEAD_DIM = 64
STATE = 128
SPAN = 256
INNER = 2560
HIGHEST = lax.Precision.HIGHEST
MASKED = -1e30
EPSILON = 1e-05


def passed_along(value, axis, steps):
    count = lax.axis_size(axis)
    first, last = (max(0, -steps), min(count, count - steps))
    return lax.ppermute(value, axis, [(source, source + steps) for source in range(first, last)])


def entering_2(value, axis, combine, identity, reverse):
    length, position = (lax.axis_size(axis), lax.axis_index(axis))
    everything = jax.tree.map(lambda part: lax.all_gather(part, axis), value)
    start = jax.tree.map(
        lambda part, zero: jnp.broadcast_to(jnp.asarray(zero, part.dtype), part.shape),
        value,
        identity,
    )

    def lap(k, before):
        at = length - 1 - k if reverse else k
        reached = at > position if reverse else at < position
        new = combine(before, jax.tree.map(lambda part: part[at], everything))
        return jax.tree.map(lambda a, b: jnp.where(reached, a, b), new, before)

    return lax.fori_loop(0, length, lap, start)


def affine(earlier, later):
    return (earlier[0] * later[0], later[0][:, None, None] * earlier[1] + later[1])


def prepare(extended, step_rows, filter_taps, filter_bias, step_bias, decay_log):
    width = filter_taps.shape[0]
    length = extended.shape[0] - width + 1
    filtered = filter_bias + filter_taps[0] * extended[0:length]
    for offset in range(1, width):
        filtered = filtered + filter_taps[offset] * extended[offset : offset + length]
    activated = jax.nn.silu(filtered)
    step_sizes = jax.nn.softplus(step_rows + step_bias[:, None])
    decay_rates = step_sizes * (-jnp.exp(decay_log))[:, None]
    blocks = length // SPAN
    cumsums = jnp.cumsum(decay_rates.reshape(HEADS, blocks, SPAN), axis=2)
    values = activated[:, :INNER].reshape(blocks, SPAN, HEADS, HEAD_DIM)
    key_side = activated[:, INNER : INNER + STATE].reshape(blocks, SPAN, STATE)
    scaled = values * step_sizes.reshape(HEADS, blocks, SPAN).transpose(1, 2, 0)[..., None]
    to_end = jnp.exp(cumsums[:, :, -1:] - cumsums)
    block_states = jnp.einsum("hcs,cshp,csn->chpn", to_end, scaled, key_side, precision=HIGHEST)
    decays = jnp.exp(cumsums[:, :, -1]).T
    return (activated, cumsums, scaled, block_states, decays)


def summarize(block_states, decays):
    product = jnp.ones((decays.shape[1],), jnp.float32)
    running = jnp.zeros(block_states.shape[1:], jnp.float32)
    running = decays[0][:, None, None] * running + block_states[0]
    product = product * decays[0]
    return (product, running)


def finish(
    activated, cumsums, scaled, block_states, decays, entering, skip_gain, gate_rows, norm_weight
):
    blocks = cumsums.shape[1]
    length = blocks * SPAN
    values = activated[:, :INNER].reshape(blocks, SPAN, HEADS, HEAD_DIM)
    key_side = activated[:, INNER : INNER + STATE].reshape(blocks, SPAN, STATE)
    query_side = activated[:, INNER + STATE :].reshape(blocks, SPAN, STATE)
    starting = []
    starting.append(entering)
    starting = jnp.stack(starting)
    scores = jnp.einsum("ctn,csn->cts", query_side, key_side, precision=HIGHEST)
    differences = cumsums[:, :, :, None] - cumsums[:, :, None, :]
    causal = jnp.tril(jnp.ones((SPAN, SPAN), dtype=bool))
    weights = scores[None] * jnp.exp(jnp.where(causal, differences, MASKED))
    inside = jnp.einsum("hcts,cshp->cthp", weights, scaled, precision=HIGHEST)
    from_state = (
        jnp.einsum("ctn,chpn->cthp", query_side, starting, precision=HIGHEST)
        * jnp.exp(cumsums).transpose(1, 2, 0)[..., None]
    )
    result = inside + from_state + skip_gain[:, None] * values
    scanned = result.reshape(length, INNER)
    gated = scanned * jax.nn.silu(gate_rows)
    inverse_rms = lax.rsqrt(jnp.mean(gated * gated, axis=1, keepdims=True) + EPSILON)
    return gated * inverse_rms * norm_weight


def body(
    conv_input,
    gate_input,
    step_input,
    filter_taps,
    filter_bias,
    step_bias,
    decay_log,
    skip_gain,
    norm_weight,
    output_weight,
    output_grad,
):
    kernel_rows = filter_taps.shape[0] - 1
    raw_rows = conv_input[0]
    before = passed_along(raw_rows[-kernel_rows:], "seq", 1)
    extended = jnp.concatenate([before, raw_rows], axis=0).astype(jnp.float32)
    gate_rows = gate_input[0].astype(jnp.float32)
    step_rows = step_input[0]
    cotangent = output_grad[0]
    tokens = cotangent.shape[0]
    primals, pull_first = jax.vjp(
        prepare, extended, step_rows, filter_taps, filter_bias, step_bias, decay_log
    )
    activated, cumsums, scaled, block_states, decays = primals
    summary, pull_summary = jax.vjp(summarize, block_states, decays)
    identity = (jnp.ones_like(summary[0]), jnp.zeros_like(summary[1]))
    _, entering = entering_2(summary, "seq", affine, identity, False)
    normed, pull_second = jax.vjp(
        finish,
        activated,
        cumsums,
        scaled,
        block_states,
        decays,
        entering,
        skip_gain,
        gate_rows,
        norm_weight,
    )
    normed_low = normed.astype(jnp.bfloat16)
    groups = lax.axis_size("dp")
    own_rows = output_weight.shape[0]
    partial_columns = lax.dot_general(
        lax.all_gather(cotangent, "dp", axis=0, tiled=True),
        output_weight,
        (((1,), (1,)), ((), ())),
        preferred_element_type=jnp.float32,
    )
    regrouped = partial_columns.reshape(groups, tokens, own_rows)
    normed_grad = lax.all_to_all(regrouped, "dp", split_axis=0, concat_axis=2, tiled=True).reshape(
        tokens, groups * own_rows
    )
    weight_piece = lax.psum_scatter(
        lax.dot_general(
            normed_low, cotangent, (((0,), (0,)), ((), ())), preferred_element_type=jnp.float32
        ),
        "dp",
        scatter_dimension=0,
        tiled=True,
    )
    weight_grad = lax.psum(weight_piece, "seq")
    second = pull_second(normed_grad)
    (
        grad_activated,
        grad_cumsums,
        grad_scaled,
        grad_states,
        grad_decays,
        grad_entering,
        grad_skip,
        grad_gate,
        grad_norm,
    ) = second
    _, end_grad = entering_2((summary[0], grad_entering), "seq", affine, identity, True)
    decay_grad = jnp.sum(end_grad * entering, axis=(1, 2))
    more_states, more_decays = pull_summary((decay_grad, end_grad))
    first = pull_first(
        (
            grad_activated,
            grad_cumsums,
            grad_scaled,
            grad_states + more_states,
            grad_decays + more_decays,
        )
    )
    grad_extended, grad_steps, grad_taps, grad_bias, grad_step_bias, grad_decay_log = first
    returned = passed_along(grad_extended[:kernel_rows], "seq", -1)
    own_part = grad_extended[kernel_rows:]
    own_part = jnp.concatenate(
        [own_part[:-kernel_rows], own_part[-kernel_rows:] + returned], axis=0
    )
    filter_part = jnp.concatenate([grad_taps, grad_bias[None]], axis=0)
    head_part = jnp.stack([grad_step_bias, grad_decay_log, grad_skip])
    filter_grads, norm_grad, head_grads = lax.psum(
        (filter_part, grad_norm, head_part), ("seq", "dp")
    )
    input_grad = own_part.astype(jnp.bfloat16)[None]
    gate_grad = grad_gate.astype(jnp.bfloat16)[None]
    step_grad = grad_steps[None]
    return (input_grad, gate_grad, step_grad, weight_grad, filter_grads, norm_grad, head_grads)


def solution(mesh):
    return jax.shard_map(
        body,
        mesh=mesh,
        in_specs=(
            P("dp", "seq", None),
            P("dp", "seq", None),
            P("dp", None, "seq"),
            P(),
            P(),
            P(),
            P(),
            P(),
            P(),
            P("dp", None),
            P("dp", "seq", None),
        ),
        out_specs=(
            P("dp", "seq", None),
            P("dp", "seq", None),
            P("dp", None, "seq"),
            P("dp", None),
            P(),
            P(),
            P(),
        ),
        check_vma=False,
    )
```

profile of v0, /device:TPU:0, one launch (start us, length us, event | category | flops | bytes accessed | tf_op | source)
XLA Modules:
  0.0 764.4 jit_solution(17478603161339498694)
XLA Ops:
  8.8 4.9 collective-permute-start
  20.2 3.0 fusion.21
  24.7 1.9 slice.95
  26.6 3.2 copy.94
  29.8 5.0 fusion.69
  34.8 3.0 all-gather.8.cloned.1.call-done
  37.9 5.5 fusion.48
  43.4 4.7 all-to-all-start
  49.6 22.7 %all-reduce.15 = f32[320]{0:T(512)S(1)} all-reduce(f32[320]{0:T(512)S(1)} %dynamic-update-slice), channel_id=3, replica_groups=mesh['seq'=8,'dp'=4] {'seq'}, use_global_device_ids=true, to_apply=%add.15 | all-reduce | flops 320 | bytes 2560
  72.4 1.8 copy.100
  75.7 3.6 all-to-all-done
  79.4 3.2 copy.93
  82.6 108.8 %all-gather.10.cloned.1.call-done = f32[320,64,128]{2,1,0:T(8,128)} async-done(((f32[40,64,128]{2,1,0:T(8,128)}), f32[320,64,128]{2,1,0:T(8,128)}) %all-gather.10.cloned.1.call-update) | async-done | bytes 10485776 | tf_op jit(solution)/shard_map/all_gather | solution.py:24
  191.4 13.2 %while.30 = (s32[]{:T(128)}, f32[40,64,128]{2,1,0:T(8,128)S(1)}, s32[]{:T(128)}, f32[8,40]{1,0:T(8,128)S(1)}, f32[8,40,64,128]{3,2,1,0:T(8,128)}, /*index=5*/s32[]{:T(128)}, s32[]{:T(128)}) while((s32[]{:T(128)}, f32[40,64,128]{2,1,0:T(8,128)S(1)}, s32[]{:T(128)}, f32[8,40]{1,0:T(8,128)S(1)}, f32[8,40,64,128]{3,2,1,0:T(8,128)}, ...), condition=%wide.region_3.4_spmd.clone, body=%wide.region_2.3_spmd.clone.sunk | while | flops 1310724 | bytes 3932745 | solution.py:37
  204.6 3.3 fusion.93
  208.0 15.5 %multiply_reduce_fusion.8 = (f32[256]{0:T(256)S(1)}, f32[256]{0:T(256)S(1)}, f32[1,256,40,64]{1,3,2,0:T(8,128)S(1)}, f32[1,256,40,64]{1,3,2,0:T(8,128)}) fusion(f32[1,256,40,64]{1,3,2,0:T(8,128)} %bitcast.259, f32[40,64]{1,0:T(8,128)S(1)} %mul.591, f32[1,256,40,64]{1,3,2,0:T(8,128)} %bitcast.262, f32[1,256,40,64]{1,3,2,0:T(8,128)S(1)} %bitcast.254, ...), kind=kOutput, calls=%fused_computation.79 | convolution fusion | flops 2030960128 | bytes 18813088 | tf_op jit(solution)/shard_map/jvp(hcts,cshp->cthp)/dot_general | solution.py:87
  223.5 2.6 broadcast_multiply_fusion.5
  227.6 4.2 fusion.44
  231.8 8.5 %fusion.86 = f32[2560,1280]{1,0:T(8,128)} fusion(bf16[256,2560]{0,1:T(8,128)(2,1)S(1)} %bitcast.268, bf16[1,256,1280]{2,1,0:T(8,128)(2,1)} %param.25), kind=kOutput, calls=%fused_computation.114 | convolution fusion | flops 1677721600 | bytes 15073280 | tf_op jit(solution)/shard_map/dot_general | solution.py:153
  240.7 3.2 convert_element_type.75
  243.9 3.7 copy.129
  247.6 15.7 %fusion.8 = (f32[40,256]{1,0:T(8,128)S(1)}, f32[40,256]{1,0:T(8,128)}, f32[256,256]{1,0:T(8,128)S(1)}) fusion(f32[40,256]{1,0:T(8,128)S(1)} %get-tuple-element.347, f32[256,256]{1,0:T(8,128)S(1)} %copy-done.19, pred[256,256]{1,0:T(8,128)(4,1)S(1)} %iota_compare_fusion, f32[256,40,64]{0,2,1:T(8,128)S(1)} %bitcast.256, f32[256,40]{0,1:T(8,128)S(1)} %fusion.106, ...), kind=kOutput, calls=%fused_computation.13 | convolution fusion | flops 2037428224 | bytes 5996544 | tf_op jit(solution)/shard_map/transpose(jvp(hcts,cshp->cthp))/dot_general | solution.py:87
  263.3 3.2 copy.101
  266.5 3.2 copy.117
  269.7 4.3 fusion.33
  274.7 3.3 copy.106
  279.6 6.0 fusion.83
  286.9 3.2 fusion.29
  290.1 90.5 %all-gather.12.cloned.1.call-done = f32[320,64,128]{2,1,0:T(8,128)} async-done(((f32[40,64,128]{2,1,0:T(8,128)}), f32[320,64,128]{2,1,0:T(8,128)}) %all-gather.12.cloned.1.call-update) | async-done | bytes 10485776 | tf_op jit(solution)/shard_map/all_gather | solution.py:24
  380.6 21.0 %while.31 = (s32[]{:T(128)}, f32[40,64,128]{2,1,0:T(8,128)S(1)}, s32[]{:T(128)}, f32[8,40]{1,0:T(8,128)}, f32[8,40,64,128]{3,2,1,0:T(8,128)}, /*index=5*/s32[]{:T(128)}, s32[]{:T(128)}, s32[]{:T(128)}, s32[]{:T(128)}) while((s32[]{:T(128)}, f32[40,64,128]{2,1,0:T(8,128)S(1)}, s32[]{:T(128)}, f32[8,40]{1,0:T(8,128)}, ...), condition=%wide.region_8.9_spmd.clone, body=%wide.region_7.8_spmd.clone.sunk | while | flops 1310728 | bytes 3932807 | solution.py:37
  386.0 2.0 fusion.138
  391.1 2.1 fusion.138
  393.9 2.1 fusion.138
  396.7 2.1 fusion.138
  399.5 1.7 fusion.138
  402.2 5.5 fusion.39
  408.7 2.5 reduce-window.16
  411.5 12.6 %multiply_reduce_fusion.5 = (f32[40]{0:T(128)S(1)}, f32[256,40]{0,1:T(8,128)S(1)}, f32[1,256,40,64]{1,3,2,0:T(8,128)}) fusion(f32[1,256,40,64]{1,3,2,0:T(8,128)} %copy-done.9, f32[1,256,40,64]{1,3,2,0:T(8,128)} %bitcast.252, f32[256,40]{0,1:T(8,128)S(1)} %fusion.106, f32[256,40]{0,1:T(8,128)S(1)} %get-tuple-element.346, ...), kind=kOutput, calls=%fused_computation.75 | convolution fusion | flops 2025707520 | bytes 10977440 | tf_op jit(solution)/shard_map/transpose(jvp(hcts,cshp->cthp))/dot_general | solution.py:87
  424.1 3.4 copy.103
  427.5 6.1 fusion.80
  433.7 6.0 multiply_reduce_fusion.4
  441.5 4.4 fusion.26
  445.9 38.5 %reduce-scatter.2.cloned.1.call-done = f32[640,1280]{1,0:T(8,128)} async-done(((f32[2560,1280]{1,0:T(8,128)}), f32[640,1280]{1,0:T(8,128)}) %reduce-scatter.2.cloned.1.call-update) | async-done | bytes 3276816 | tf_op jit(solution)/shard_map/reduce_scatter | solution.py:152
  484.4 2.7 broadcast_multiply_fusion.3
  490.8 2.4 collective-permute-done.1
  494.4 120.0 %all-reduce.22.cloned.1.call-done = (f32[5,2816]{1,0:T(8,128)}, f32[2560]{0:T(1024)}, f32[3,40]{1,0:T(4,128)}) async-done(((f32[5,2816]{1,0:T(8,128)}, f32[2560]{0:T(1024)}, f32[3,40]{1,0:T(4,128)}), (f32[5,2816]{1,0:T(8,128)}, f32[2560]{0:T(1024)}, f32[3,40]{1,0:T(4,128)})) %all-reduce.22.cloned.1.call-update) | async-done | bytes 67056 | tf_op jit(solution)/shard_map/psum | solution.py:193
  614.4 137.1 %all-reduce.20.cloned.1.call-done = f32[640,1280]{1,0:T(8,128)} async-done(((f32[640,1280]{1,0:T(8,128)}), f32[640,1280]{1,0:T(8,128)}) %all-reduce.20.cloned.1.call-update) | async-done | bytes 3276816 | tf_op jit(solution)/shard_map/psum | solution.py:160
  751.5 4.0 copy.175
  (174 shorter events, 51.1 us)
Async XLA Ops:
  7.2 30.7 %copy-start = (bf16[640,1280]{1,0:T(8,128)(2,1)S(1)}, bf16[640,1280]{1,0:T(8,128)(2,1)}, u32[]{:S(2)}) copy-start(bf16[640,1280]{1,0:T(8,128)(2,1)} %param.24) | copy-start | bytes 4915204
  7.2 12.7 %copy-start.16 = (bf16[1,256,2816]{2,1,0:T(8,128)(2,1)S(1)}, bf16[1,256,2816]{2,1,0:T(8,128)(2,1)}, u32[]{:S(2)}) copy-start(bf16[1,256,2816]{2,1,0:T(8,128)(2,1)} %param.15) | copy-start | bytes 4325380
  7.2 30.7 %all-gather.8.cloned.1.call-start = ((), (), s32[]{:S(2)}) async-start(), calls=%async_computation.4 | async-start | bytes 3276800 | tf_op jit(solution)/shard_map/all_gather | solution.py:143
  7.9 183.4 %all-gather.10.cloned.1.call-start = ((), (), s32[]{:S(2)}) async-start(), calls=%async_computation.5 | async-start | bytes 11796480 | tf_op jit(solution)/shard_map/all_gather | solution.py:24
  8.8 11.1 %collective-permute-start = (bf16[3,2816]{1,0:T(4,128)(2,1)S(1)}, bf16[3,2816]{1,0:T(4,128)(2,1)S(1)}, u32[]{:S(2)}, u32[]{:S(2)}) collective-permute-start(bf16[3,2816]{1,0:T(4,128)(2,1)S(1)} %slice_bitcast_fusion), channel_id=1, source_target_pairs={{0,4},{4,8},{8,12},{12,16},{16,20},{20,24},{24,28},{1,5},{5,9},{9,... | collective-permute-start | bytes 50696 | tf_op jit(solution)/shard_map/ppermute | solution.py:19
  16.5 3.7 copy-start.24
  20.2 3.0 copy-start.2
  23.2 1.6 copy-start.12
  43.4 4.8 copy-start.31
  43.4 29.1 %copy-start.13 = (bf16[1,256,2560]{2,1,0:T(8,128)(2,1)S(1)}, bf16[1,256,2560]{2,1,0:T(8,128)(2,1)}, u32[]{:S(2)}) copy-start(bf16[1,256,2560]{2,1,0:T(8,128)(2,1)} %param.16) | copy-start | bytes 3932164
  43.4 36.0 %all-to-all-start = ((f32[4,256,640]{2,1,0:T(8,128)}), f32[4,256,640]{2,1,0:T(8,128)}, u32[]{:S(2)}, u32[]{:S(2)}) async-start(f32[4,256,640]{2,1,0:T(8,128)} %bitcast.271), calls=%async_computation | async-start | bytes 5242880 | tf_op jit(solution)/shard_map/all_to_all | solution.py:149
  48.0 26.2 %copy-start.22 = (f32[2560]{0:T(1024)S(1)}, f32[2560]{0:T(1024)}, u32[]{:S(2)}) copy-start(f32[2560]{0:T(1024)} %param.23) | copy-start | bytes 30724
  48.0 332.6 %all-gather.12.cloned.1.call-start = ((), (), s32[]{:S(2)}) async-start(), calls=%async_computation.6 | async-start | bytes 11796480 | tf_op jit(solution)/shard_map/all_gather | solution.py:24
  75.7 132.2 %copy-start.18 = (f32[256,256]{1,0:T(8,128)}, f32[256,256]{1,0:T(8,128)S(1)}, u32[]{:S(2)}) copy-start(f32[256,256]{1,0:T(8,128)S(1)} %fusion.98) | copy-start | bytes 786436
  204.6 18.9 %copy-start.27 = (f32[8,40]{1,0:T(8,128)}, f32[8,40]{1,0:T(8,128)S(1)}, u32[]{:S(2)}) copy-start(f32[8,40]{1,0:T(8,128)S(1)} %get-tuple-element.516) | copy-start | bytes 3844
  204.6 3.3 copy-start.4
  204.6 3.3 copy-start.29
  207.9 15.6 %copy-start.15 = (f32[256,40,64]{0,2,1:T(8,128)}, f32[256,40,64]{0,2,1:T(8,128)S(1)}, u32[]{:S(2)}) copy-start(f32[256,40,64]{0,2,1:T(8,128)S(1)} %fusion.93) | copy-start | bytes 7864324
  207.9 15.6 %copy-start.7 = (f32[1,256,4,640]{1,3,2,0:T(8,128)S(1)}, f32[1,256,4,640]{1,3,2,0:T(8,128)}, u32[]{:S(2)}) copy-start(f32[1,256,4,640]{1,3,2,0:T(8,128)} %copy.93) | copy-start | bytes 7864324
  208.0 15.6 %copy-start.11 = (f32[1,256,2560]{1,2,0:T(8,128)S(1)}, f32[1,256,2560]{1,2,0:T(8,128)}, u32[]{:S(2)}) copy-start(f32[1,256,2560]{1,2,0:T(8,128)} %copy.100) | copy-start | bytes 7864324
  226.1 1.5 copy-start.9
  231.8 252.6 %reduce-scatter.2.cloned.1.call-start = ((), (), s32[]{:S(2)}) async-start(), calls=%async_computation.2 | async-start | bytes 16384000 | tf_op jit(solution)/shard_map/reduce_scatter | solution.py:152
  240.4 374.0 %all-reduce.22.cloned.1.call-start = ((), (), s32[]{:S(2)}) async-start(), calls=%async_computation.7 | async-start | bytes 208896 | tf_op jit(solution)/shard_map/psum | solution.py:193
  240.7 7.0 copy-start.19
  243.9 3.8 copy-start.5
  243.9 3.8 copy-start.10
  277.9 8.9 %copy-start.6 = (f32[1,256,40,64]{1,3,2,0:T(8,128)S(1)}, f32[1,256,40,64]{1,3,2,0:T(8,128)}, u32[]{:S(2)}) copy-start(f32[1,256,40,64]{1,3,2,0:T(8,128)} %get-tuple-element.358) | copy-start | bytes 7864324
  277.9 8.9 %copy-start.8 = (f32[1,256,4,640]{1,3,2,0:T(8,128)S(1)}, f32[1,256,4,640]{1,3,2,0:T(8,128)}, u32[]{:S(2)}) copy-start(f32[1,256,4,640]{1,3,2,0:T(8,128)} %copy.93) | copy-start | bytes 7864324
  402.2 6.4 copy-start.23
  402.2 9.3 %copy-start.20 = (f32[256,256]{1,0:T(8,128)S(1)}, f32[256,256]{1,0:T(8,128)}, u32[]{:S(2)}) copy-start(f32[256,256]{1,0:T(8,128)} %copy-done.18) | copy-start | bytes 786436
  427.5 6.1 copy-start.3
  433.6 6.2 copy-start.17
  433.6 6.2 copy-start.26
  433.7 6.4 copy-start.30
  433.7 7.8 %copy-start.14 = (bf16[1,256,2560]{2,1,0:T(8,128)(2,1)S(1)}, bf16[1,256,2560]{2,1,0:T(8,128)(2,1)}, u32[]{:S(2)}) copy-start(bf16[1,256,2560]{2,1,0:T(8,128)(2,1)} %param.16) | copy-start | bytes 3932164
  441.4 310.1 %all-reduce.20.cloned.1.call-start = ((), (), s32[]{:S(2)}) async-start(), calls=%async_computation.3 | async-start | bytes 6553600 | tf_op jit(solution)/shard_map/psum | solution.py:160
  487.2 5.9 collective-permute-start.1
  751.5 5.8 copy-start.1
  751.5 4.0 copy-start.21
  751.5 4.6 copy-start.25
  751.5 5.2 copy-start.28
Sparse Core Ops, SparseCore 0:
  9.6 28.2 all-gather.7
  40.6 150.7 all-gather.9
  231.9 148.6 all-gather.11
  383.1 101.2 reduce-scatter.1
  490.8 123.6 all-reduce.21
  617.9 133.5 all-reduce.19
where the time goes:
time: 772 us; the launch traced here: 764 us
  waiting for transfers between devices  505 us (65%)
  matrix products  92.2 us (12%)
  other arithmetic  69.3 us (9%)
  local copies, waits for them, and re-layouts  47.8 us (6%)
  blocking collectives  22.7 us (3%)
  between operations  15.6 us (2%)
  starting transfers between devices  11.3 us (1%)
    all_gather x2, waiting for transfers between devices, entering_2(): everything = jax.tree.map(lambda part: lax.all_gather(part, axis), value)  199 us
    psum x1, waiting for transfers between devices, body(): weight_grad = lax.psum(weight_piece, 'seq')  137 us
    psum x1, waiting for transfers between devices, body(): lax.psum((filter_part, grad_norm, head_part), ('seq', 'dp'))  120 us
    dot_general x3, matrix products, finish(): inside = jnp.einsum('hcts,cshp->cthp', weights, scaled, precision=HIGHEST)  43.8 us
    reduce_scatter x1, waiting for transfers between devices, body(): lax.psum_scatter(lax.dot_general(normed_low, cotangent, (((0,), (0,)), ((...  38.5 us
    select_n x16, other arithmetic, lap(): return jax.tree.map(lambda a, b: jnp.where(reached, a, b), new, before)  27.8 us
    unnamed x1, blocking collectives  22.7 us
    dot_general x3, matrix products, prepare(): jnp.einsum('hcs,cshp,csn->chpn', to_end, scaled, key_side, precision=HIGH...  16.7 us
  transfers between devices with their start and end apart: 9, of which 8 were waited for; matrix products, arithmetic and copies ran while one was open for 21% of the time, Pallas kernels for 0%

commit v1 on v0

--- a/solution.py
+++ b/solution.py
@@ -191,7 +191,7 @@
     filter_part = jnp.concatenate([grad_taps, grad_bias[None]], axis=0)
     head_part = jnp.stack([grad_step_bias, grad_decay_log, grad_skip])
     filter_grads, norm_grad, head_grads = lax.psum(
-        (filter_part, grad_norm, head_part), ("seq", "dp")
+        lax.psum((filter_part, grad_norm, head_part), "dp"), "seq"
     )
     input_grad = own_part.astype(jnp.bfloat16)[None]
     gate_grad = grad_gate.astype(jnp.bfloat16)[None]

time: 772 us -> 802 us (1.039)
  waiting for transfers between devices: 505 us -> 542 us
    reduce_scatter x1, waiting for transfers between devices: 38.5 us -> 103 us  [body(): lax.psum_scatter(lax.dot_general(normed_low, cotangent, (((0,), (0,)), ((...]
    psum x1 -> x2, waiting for transfers between devices: 120 us -> 79.4 us  [the longest x1 65.4 us: body(): lax.psum(lax.psum((filter_part, grad_norm, head_part), 'dp'), 'seq')]
    all_gather x2, waiting for transfers between devices: 199 us -> 214 us  [entering_2(): everything = jax.tree.map(lambda part: lax.all_gather(part, axis), value)]
  transfers between devices with their start and end apart: 9 -> 10, of which waited for: 8 -> 9; matrix products, arithmetic and copies ran while one was open for 21% -> 12% of each run, Pallas kernels for 0% -> 0%
where the time goes in v1:
time: 802 us; the launch traced here: 795 us
  waiting for transfers between devices  542 us (68%)
  matrix products  92.4 us (12%)
  other arithmetic  67.9 us (8%)
  local copies, waits for them, and re-layouts  41.9 us (5%)
  blocking collectives  22.8 us (3%)
  between operations  16.2 us (2%)
  starting transfers between devices  11.8 us (1%)
    all_gather x2, waiting for transfers between devices, entering_2(): everything = jax.tree.map(lambda part: lax.all_gather(part, axis), value)  214 us
    psum x1, waiting for transfers between devices, body(): weight_grad = lax.psum(weight_piece, 'seq')  136 us
    reduce_scatter x1, waiting for transfers between devices, body(): lax.psum_scatter(lax.dot_general(normed_low, cotangent, (((0,), (0,)), ((...  103 us
    psum x1, waiting for transfers between devices, body(): lax.psum(lax.psum((filter_part, grad_norm, head_part), 'dp'), 'seq')  65.4 us
    dot_general x3, matrix products, finish(): inside = jnp.einsum('hcts,cshp->cthp', weights, scaled, precision=HIGHEST)  44.7 us
    select_n x16, other arithmetic, lap(): return jax.tree.map(lambda a, b: jnp.where(reached, a, b), new, before)  25.9 us
    unnamed x1, blocking collectives  22.8 us
  transfers between devices with their start and end apart: 10, of which 9 were waited for; matrix products, arithmetic and copies ran while one was open for 12% of the time, Pallas kernels for 0%

profile of v1, /device:TPU:0, one launch (start us, length us, event | category | flops | bytes accessed | tf_op | source)
XLA Modules:
  0.0 795.2 jit_solution(4669100832692535764)
XLA Ops:
  8.8 4.9 collective-permute-start
  20.3 3.0 fusion.21
  23.3 1.7 copy-done.12
  25.0 1.8 slice.95
  26.8 3.3 copy.94
  30.1 5.0 fusion.69
  35.1 2.7 all-gather.8.cloned.1.call-done
  37.9 5.5 fusion.48
  43.3 4.7 all-to-all-start
  49.6 22.8 %all-reduce.15 = f32[320]{0:T(512)S(1)} all-reduce(f32[320]{0:T(512)S(1)} %dynamic-update-slice), channel_id=3, replica_groups=mesh['seq'=8,'dp'=4] {'seq'}, use_global_device_ids=true, to_apply=%add.15 | all-reduce | flops 320 | bytes 2560
  72.5 1.9 copy.100
  75.8 3.5 all-to-all-done
  79.3 3.2 copy.93
  82.6 108.8 %all-gather.10.cloned.1.call-done = f32[320,64,128]{2,1,0:T(8,128)} async-done(((f32[40,64,128]{2,1,0:T(8,128)}), f32[320,64,128]{2,1,0:T(8,128)}) %all-gather.10.cloned.1.call-update) | async-done | bytes 10485776 | tf_op jit(solution)/shard_map/all_gather | solution.py:24
  191.4 13.2 %while.30 = (s32[]{:T(128)}, f32[40,64,128]{2,1,0:T(8,128)S(1)}, s32[]{:T(128)}, f32[8,40]{1,0:T(8,128)S(1)}, f32[8,40,64,128]{3,2,1,0:T(8,128)}, /*index=5*/s32[]{:T(128)}, s32[]{:T(128)}) while((s32[]{:T(128)}, f32[40,64,128]{2,1,0:T(8,128)S(1)}, s32[]{:T(128)}, f32[8,40]{1,0:T(8,128)S(1)}, f32[8,40,64,128]{3,2,1,0:T(8,128)}, ...), condition=%wide.region_3.4_spmd.clone, body=%wide.region_2.3_spmd.clone.sunk | while | flops 1310724 | bytes 3932745 | solution.py:37
  204.6 3.3 fusion.93
  207.9 15.5 %multiply_reduce_fusion.8 = (f32[256]{0:T(256)S(1)}, f32[256]{0:T(256)S(1)}, f32[1,256,40,64]{1,3,2,0:T(8,128)S(1)}, f32[1,256,40,64]{1,3,2,0:T(8,128)}) fusion(f32[1,256,40,64]{1,3,2,0:T(8,128)} %bitcast.259, f32[40,64]{1,0:T(8,128)S(1)} %mul.591, f32[1,256,40,64]{1,3,2,0:T(8,128)} %bitcast.262, f32[1,256,40,64]{1,3,2,0:T(8,128)S(1)} %bitcast.253, ...), kind=kOutput, calls=%fused_computation.79 | convolution fusion | flops 2030960128 | bytes 18813088 | tf_op jit(solution)/shard_map/jvp(hcts,cshp->cthp)/dot_general | solution.py:87
  223.5 3.5 broadcast_multiply_fusion.5
  227.0 5.0 fusion.44
  232.5 3.3 convert_element_type.75
  235.8 15.8 %fusion.8 = (f32[40,256]{1,0:T(8,128)S(1)}, f32[40,256]{1,0:T(8,128)S(1)}, f32[256,256]{1,0:T(8,128)S(1)}) fusion(f32[40,256]{1,0:T(8,128)S(1)} %get-tuple-element.350, f32[256,256]{1,0:T(8,128)S(1)} %fusion.98, pred[256,256]{1,0:T(8,128)(4,1)S(1)} %iota_compare_fusion, f32[256,40,64]{0,2,1:T(8,128)S(1)} %bitcast.255, f32[256,40]{0,1:T(8,128)S(1)} %fusion.106, ...), kind=kOutput, calls=%fused_computation.13 | convolution fusion | flops 2037428224 | bytes 5996544 | tf_op jit(solution)/shard_map/transpose(jvp(hcts,cshp->cthp))/dot_general | solution.py:87
  251.6 3.3 copy.101
  254.9 3.4 copy.117
  258.3 4.3 fusion.33
  263.2 1.6 fusion.101
  264.9 6.0 fusion.83
  272.2 3.3 fusion.29
  275.5 105.4 %all-gather.12.cloned.1.call-done = f32[320,64,128]{2,1,0:T(8,128)} async-done(((f32[40,64,128]{2,1,0:T(8,128)}), f32[320,64,128]{2,1,0:T(8,128)}) %all-gather.12.cloned.1.call-update) | async-done | bytes 10485776 | tf_op jit(solution)/shard_map/all_gather | solution.py:24
  380.9 13.3 %while.31 = (s32[]{:T(128)}, f32[40,64,128]{2,1,0:T(8,128)S(1)}, s32[]{:T(128)}, f32[8,40]{1,0:T(8,128)S(1)}, f32[8,40,64,128]{3,2,1,0:T(8,128)}, /*index=5*/s32[]{:T(128)}, s32[]{:T(128)}, s32[]{:T(128)}, s32[]{:T(128)}) while((s32[]{:T(128)}, f32[40,64,128]{2,1,0:T(8,128)S(1)}, s32[]{:T(128)}, f32[8,40]{1,0:T(8,128)S(1)}, ...), condition=%wide.region_8.9_spmd.clone, body=%wide.region_7.8_spmd.clone.sunk | while | flops 1310728 | bytes 3932807 | solution.py:37
  382.6 1.6 fusion.138
  385.9 1.6 fusion.138
  390.9 1.6 fusion.138
  396.0 4.7 fusion.39
  401.8 2.7 reduce-window.16
  404.7 6.0 fusion.80
  410.8 13.3 %multiply_reduce_fusion.5 = (f32[40]{0:T(128)}, f32[256,40]{0,1:T(8,128)S(1)}, f32[1,256,40,64]{1,3,2,0:T(8,128)}) fusion(f32[1,256,40,64]{1,3,2,0:T(8,128)} %get-tuple-element.345, f32[1,256,40,64]{1,3,2,0:T(8,128)} %bitcast.252, f32[256,40]{0,1:T(8,128)S(1)} %fusion.106, f32[256,40]{0,1:T(8,128)S(1)} %copy-done.19, ...), kind=kOutput, calls=%fused_computation.75 | convolution fusion | flops 2025707520 | bytes 10977440 | tf_op jit(solution)/shard_map/transpose(jvp(hcts,cshp->cthp))/dot_general | solution.py:87
  425.6 3.5 copy.103
  429.1 5.8 multiply_reduce_fusion.4
  436.6 8.1 %fusion.86 = f32[2560,1280]{1,0:T(8,128)} fusion(bf16[256,2560]{0,1:T(8,128)(2,1)} %bitcast.268, bf16[1,256,1280]{2,1,0:T(8,128)(2,1)} %param.25), kind=kOutput, calls=%fused_computation.114 | convolution fusion | flops 1677721600 | bytes 15073280 | tf_op jit(solution)/shard_map/dot_general | solution.py:153
  444.8 3.7 copy.129
  448.5 2.1 copy.106
  450.6 14.0 %all-reduce.26.cloned.1.call-done = (f32[5,2816]{1,0:T(8,128)}, f32[2560]{0:T(1024)}, f32[3,40]{1,0:T(4,128)}) async-done(((f32[5,2816]{1,0:T(8,128)}, f32[2560]{0:T(1024)}, f32[3,40]{1,0:T(4,128)}), (f32[5,2816]{1,0:T(8,128)}, f32[2560]{0:T(1024)}, f32[3,40]{1,0:T(4,128)})) %all-reduce.26.cloned.1.call-update) | async-done | bytes 67056 | tf_op jit(solution)/shard_map/psum | solution.py:194
  464.7 4.6 fusion.26
  469.3 102.9 %reduce-scatter.2.cloned.1.call-done = f32[640,1280]{1,0:T(8,128)} async-done(((f32[2560,1280]{1,0:T(8,128)}), f32[640,1280]{1,0:T(8,128)}) %reduce-scatter.2.cloned.1.call-update) | async-done | bytes 3276816 | tf_op jit(solution)/shard_map/reduce_scatter | solution.py:152
  577.2 2.0 collective-permute-done.1
  580.5 65.4 %all-reduce.24.cloned.1.call-done = (f32[5,2816]{1,0:T(8,128)}, f32[2560]{0:T(1024)}, f32[3,40]{1,0:T(4,128)}) async-done(((f32[5,2816]{1,0:T(8,128)}, f32[2560]{0:T(1024)}, f32[3,40]{1,0:T(4,128)}), (f32[5,2816]{1,0:T(8,128)}, f32[2560]{0:T(1024)}, f32[3,40]{1,0:T(4,128)})) %all-reduce.24.cloned.1.call-update) | async-done | bytes 67056 | tf_op jit(solution)/shard_map/psum | solution.py:193
  645.9 136.2 %all-reduce.22.cloned.1.call-done = f32[640,1280]{1,0:T(8,128)} async-done(((f32[640,1280]{1,0:T(8,128)}), f32[640,1280]{1,0:T(8,128)}) %all-reduce.22.cloned.1.call-update) | async-done | bytes 3276816 | tf_op jit(solution)/shard_map/psum | solution.py:160
  782.1 4.0 copy.178
  (227 shorter events, 48.3 us)
Async XLA Ops:
  7.2 30.7 %copy-start = (bf16[640,1280]{1,0:T(8,128)(2,1)S(1)}, bf16[640,1280]{1,0:T(8,128)(2,1)}, u32[]{:S(2)}) copy-start(bf16[640,1280]{1,0:T(8,128)(2,1)} %param.24) | copy-start | bytes 4915204
  7.2 12.7 %copy-start.16 = (bf16[1,256,2816]{2,1,0:T(8,128)(2,1)S(1)}, bf16[1,256,2816]{2,1,0:T(8,128)(2,1)}, u32[]{:S(2)}) copy-start(bf16[1,256,2816]{2,1,0:T(8,128)(2,1)} %param.15) | copy-start | bytes 4325380
  7.2 30.7 %all-gather.8.cloned.1.call-start = ((), (), s32[]{:S(2)}) async-start(), calls=%async_computation.4 | async-start | bytes 3276800 | tf_op jit(solution)/shard_map/all_gather | solution.py:143
  7.9 183.4 %all-gather.10.cloned.1.call-start = ((), (), s32[]{:S(2)}) async-start(), calls=%async_computation.5 | async-start | bytes 11796480 | tf_op jit(solution)/shard_map/all_gather | solution.py:24
  8.8 11.1 %collective-permute-start = (bf16[3,2816]{1,0:T(4,128)(2,1)S(1)}, bf16[3,2816]{1,0:T(4,128)(2,1)S(1)}, u32[]{:S(2)}, u32[]{:S(2)}) collective-permute-start(bf16[3,2816]{1,0:T(4,128)(2,1)S(1)} %slice_bitcast_fusion), channel_id=1, source_target_pairs={{0,4},{4,8},{8,12},{12,16},{16,20},{20,24},{24,28},{1,5},{5,9},{9,... | collective-permute-start | bytes 50696 | tf_op jit(solution)/shard_map/ppermute | solution.py:19
  17.8 5.4 copy-start.45
  18.8 11.3 %copy-start.18 = (f32[256,40]{0,1:T(8,128)}, f32[256,40]{0,1:T(8,128)S(1)}, u32[]{:S(2)}) copy-start(f32[256,40]{0,1:T(8,128)S(1)} %get-tuple-element.349) | copy-start | bytes 122884
  18.8 217.0 %copy-start.35 = (f32[40,256]{1,0:T(8,128)}, f32[40,256]{1,0:T(8,128)S(1)}, u32[]{:S(2)}) copy-start(f32[40,256]{1,0:T(8,128)S(1)} %get-tuple-element.350) | copy-start | bytes 122884
  43.3 29.1 %copy-start.13 = (bf16[1,256,2560]{2,1,0:T(8,128)(2,1)S(1)}, bf16[1,256,2560]{2,1,0:T(8,128)(2,1)}, u32[]{:S(2)}) copy-start(bf16[1,256,2560]{2,1,0:T(8,128)(2,1)} %param.16) | copy-start | bytes 3932164
  43.3 36.0 %all-to-all-start = ((f32[4,256,640]{2,1,0:T(8,128)}), f32[4,256,640]{2,1,0:T(8,128)}, u32[]{:S(2)}, u32[]{:S(2)}) async-start(f32[4,256,640]{2,1,0:T(8,128)} %bitcast.271), calls=%async_computation | async-start | bytes 5242880 | tf_op jit(solution)/shard_map/all_to_all | solution.py:149
  48.0 26.3 %copy-start.33 = (f32[2560]{0:T(1024)S(1)}, f32[2560]{0:T(1024)}, u32[]{:S(2)}) copy-start(f32[2560]{0:T(1024)} %param.23) | copy-start | bytes 30724
  48.0 332.9 %all-gather.12.cloned.1.call-start = ((), (), s32[]{:S(2)}) async-start(), calls=%async_computation.6 | async-start | bytes 11796480 | tf_op jit(solution)/shard_map/all_gather | solution.py:24
  74.4 161.4 %copy-start.31 = (pred[256,256]{1,0:T(8,128)(4,1)}, pred[256,256]{1,0:T(8,128)(4,1)S(1)}, u32[]{:S(2)}) copy-start(pred[256,256]{1,0:T(8,128)(4,1)S(1)} %iota_compare_fusion) | copy-start | bytes 196612
  75.8 160.0 %copy-start.20 = (f32[256,256]{1,0:T(8,128)}, f32[256,256]{1,0:T(8,128)S(1)}, u32[]{:S(2)}) copy-start(f32[256,256]{1,0:T(8,128)S(1)} %fusion.98) | copy-start | bytes 786436
  207.9 15.6 %copy-start.15 = (f32[256,40,64]{0,2,1:T(8,128)}, f32[256,40,64]{0,2,1:T(8,128)S(1)}, u32[]{:S(2)}) copy-start(f32[256,40,64]{0,2,1:T(8,128)S(1)} %fusion.93) | copy-start | bytes 7864324
  207.9 15.6 %copy-start.9 = (f32[1,256,4,640]{1,3,2,0:T(8,128)S(1)}, f32[1,256,4,640]{1,3,2,0:T(8,128)}, u32[]{:S(2)}) copy-start(f32[1,256,4,640]{1,3,2,0:T(8,128)} %copy.93) | copy-start | bytes 7864324
  207.9 15.6 %copy-start.11 = (f32[1,256,2560]{1,2,0:T(8,128)S(1)}, f32[1,256,2560]{1,2,0:T(8,128)}, u32[]{:S(2)}) copy-start(f32[1,256,2560]{1,2,0:T(8,128)} %copy.100) | copy-start | bytes 7864324
  223.5 48.7 %copy-start.37 = (f32[256]{0:T(256)}, f32[256]{0:T(256)S(1)}, u32[]{:S(2)}) copy-start(f32[256]{0:T(256)S(1)} %get-tuple-element.359) | copy-start | bytes 3076
  223.5 48.7 %copy-start.39 = (f32[256]{0:T(256)}, f32[256]{0:T(256)S(1)}, u32[]{:S(2)}) copy-start(f32[256]{0:T(256)S(1)} %get-tuple-element.360) | copy-start | bytes 3076
  232.0 232.6 %all-reduce.26.cloned.1.call-start = ((), (), s32[]{:S(2)}) async-start(), calls=%async_computation.8 | async-start | bytes 208896 | tf_op jit(solution)/shard_map/psum | solution.py:194
  263.2 8.9 %copy-start.7 = (f32[1,256,40,64]{1,3,2,0:T(8,128)S(1)}, f32[1,256,40,64]{1,3,2,0:T(8,128)}, u32[]{:S(2)}) copy-start(f32[1,256,40,64]{1,3,2,0:T(8,128)} %get-tuple-element.361) | copy-start | bytes 7864324
  263.2 9.0 %copy-start.10 = (f32[1,256,4,640]{1,3,2,0:T(8,128)S(1)}, f32[1,256,4,640]{1,3,2,0:T(8,128)}, u32[]{:S(2)}) copy-start(f32[1,256,4,640]{1,3,2,0:T(8,128)} %copy.93) | copy-start | bytes 7864324
  396.0 5.0 copy-start.46
  396.0 8.7 %copy-start.19 = (f32[256,40]{0,1:T(8,128)S(1)}, f32[256,40]{0,1:T(8,128)}, u32[]{:S(2)}) copy-start(f32[256,40]{0,1:T(8,128)} %copy-done.18) | copy-start | bytes 122884
  400.7 10.1 %copy-start.21 = (f32[256,256]{1,0:T(8,128)S(1)}, f32[256,256]{1,0:T(8,128)}, u32[]{:S(2)}) copy-start(f32[256,256]{1,0:T(8,128)} %copy-done.20) | copy-start | bytes 786436
  400.7 10.1 %copy-start.32 = (pred[256,256]{1,0:T(8,128)(4,1)S(1)}, pred[256,256]{1,0:T(8,128)(4,1)}, u32[]{:S(2)}) copy-start(pred[256,256]{1,0:T(8,128)(4,1)} %copy-done.31) | copy-start | bytes 196612
  400.7 10.1 %copy-start.36 = (f32[40,256]{1,0:T(8,128)S(1)}, f32[40,256]{1,0:T(8,128)}, u32[]{:S(2)}) copy-start(f32[40,256]{1,0:T(8,128)} %copy-done.35) | copy-start | bytes 122884
  410.8 13.5 %copy-start.17 = (f32[1,40,256]{2,1,0:T(8,128)S(1)}, f32[1,40,256]{2,1,0:T(8,128)}, u32[]{:S(2)}) copy-start(f32[1,40,256]{2,1,0:T(8,128)} %param.17) | copy-start | bytes 122884
  410.8 13.5 %copy-start.43 = (f32[40]{0:T(128)S(1)}, f32[40]{0:T(128)}, u32[]{:S(2)}) copy-start(f32[40]{0:T(128)} %param.20) | copy-start | bytes 484
  410.8 13.5 %copy-start.48 = (f32[40]{0:T(128)S(1)}, f32[40]{0:T(128)}, u32[]{:S(2)}) copy-start(f32[40]{0:T(128)} %copy-done.47) | copy-start | bytes 484
  410.8 14.3 %copy-start.55 = (f32[40]{0:T(128)S(1)}, f32[40]{0:T(128)}, u32[]{:S(2)}) copy-start(f32[40]{0:T(128)} %param.21) | copy-start | bytes 484
  429.1 6.6 copy-start.51
  429.1 6.6 copy-start.53
  429.1 6.6 copy-start.54
  436.3 136.0 %reduce-scatter.2.cloned.1.call-start = ((), (), s32[]{:S(2)}) async-start(), calls=%async_computation.2 | async-start | bytes 16384000 | tf_op jit(solution)/shard_map/reduce_scatter | solution.py:152
  444.7 201.2 %all-reduce.24.cloned.1.call-start = ((), (), s32[]{:S(2)}) async-start(), calls=%async_computation.7 | async-start | bytes 208896 | tf_op jit(solution)/shard_map/psum | solution.py:193
  448.5 16.2 %copy-start.34 = (f32[2560]{0:T(1024)S(1)}, f32[2560]{0:T(1024)}, u32[]{:S(2)}) copy-start(f32[2560]{0:T(1024)} %param.23) | copy-start | bytes 30724
  448.5 16.2 %copy-start.38 = (f32[256]{0:T(256)S(1)}, f32[256]{0:T(256)}, u32[]{:S(2)}) copy-start(f32[256]{0:T(256)} %copy-done.37) | copy-start | bytes 3076
  448.5 16.2 %copy-start.40 = (f32[256]{0:T(256)S(1)}, f32[256]{0:T(256)}, u32[]{:S(2)}) copy-start(f32[256]{0:T(256)} %copy-done.39) | copy-start | bytes 3076
  464.6 317.4 %all-reduce.22.cloned.1.call-start = ((), (), s32[]{:S(2)}) async-start(), calls=%async_computation.3 | async-start | bytes 6553600 | tf_op jit(solution)/shard_map/psum | solution.py:160
  469.3 103.0 %copy-start.14 = (f32[256,2816]{1,0:T(8,128)S(1)}, f32[256,2816]{1,0:T(8,128)}, u32[]{:S(2)}) copy-start(f32[256,2816]{1,0:T(8,128)} %get-tuple-element.341) | copy-start | bytes 8650756
  469.3 103.0 %copy-start.23 = (f32[2816]{0:T(1024)S(1)}, f32[2816]{0:T(1024)}, u32[]{:S(2)}) copy-start(f32[2816]{0:T(1024)} %copy-done.22) | copy-start | bytes 33796
  469.3 103.0 %copy-start.25 = (f32[2816]{0:T(1024)S(1)}, f32[2816]{0:T(1024)}, u32[]{:S(2)}) copy-start(f32[2816]{0:T(1024)} %copy-done.24) | copy-start | bytes 33796
  469.3 103.0 %copy-start.27 = (f32[2816]{0:T(1024)S(1)}, f32[2816]{0:T(1024)}, u32[]{:S(2)}) copy-start(f32[2816]{0:T(1024)} %copy-done.26) | copy-start | bytes 33796
  469.3 103.0 %copy-start.29 = (f32[2816]{0:T(1024)S(1)}, f32[2816]{0:T(1024)}, u32[]{:S(2)}) copy-start(f32[2816]{0:T(1024)} %copy-done.28) | copy-start | bytes 33796
  573.3 5.9 collective-permute-start.1
  782.1 5.8 copy-start.1
  782.1 5.2 copy-start.50
  (19 other events, 56.2 us)
Sparse Core Ops, SparseCore 0:
  9.6 28.2 all-gather.7
  40.6 150.7 all-gather.9
  232.1 148.6 all-gather.11
  436.4 28.1 all-reduce.25
  467.1 105.1 reduce-scatter.1
  575.7 70.1 all-reduce.23
  649.5 132.5 all-reduce.21
